TPU v7x, 256 devices: a whole 4x4x8 slice. The times are simulated.
256 devices in a mesh: row: 8 (over x, core), col: 32 (over y, z).
Axes of the slice: x: 4, y: 4, z: 8, core: 2. Of those that a mesh axis runs over, the one named last changes fastest.
Arguments:
- matrix: float32 [2048, 65536], P('col', 'row'), may hold values from -6 to 6
- basis: float32 [65536, 512], P(('row', 'col')), may hold values from -0.0234375 to 0.0234375
Outputs:
- root: float32 [512, 512], P('row', 'col')
- right: float32 [2048, 512], P('col')
All inputs are finite; a program needn't handle non-finite values.
Results may differ from a plain program's by a relative error of at most 0.00018.
Values sent between devices are 32-bit elements; how exact they have to be, the bound alone decides.
No kernel may reach another device: no remote copies, remote signals or barrier semaphores. Data moves between devices by JAX's collectives and lax.ppermute only.
A program may use at most 64 MiB of HBM per device.

v0:
```python
import jax
import jax.numpy as jnp
from jax import lax
from jax.sharding import PartitionSpec as P

ITERS = 8


def copy_for_each(value, axis):
    copies = jnp.broadcast_to(value, (lax.axis_size(axis), *value.shape))
    return lax.all_to_all(copies, axis, split_axis=0, concat_axis=0, tiled=True)


def over_copies(value, axis):
    return copy_for_each(value, axis).sum(axis=0)


def cut_along(value, dim, size):
    before, after = (value.shape[:dim], value.shape[dim + 1 :])
    return jnp.moveaxis(value.reshape(*before, size, -1, *after), dim, 0)


def summed_on_arrival(value, axis, dim):
    size = lax.axis_size(axis)
    tiles = lax.all_to_all(cut_along(value, dim, size), axis, 0, 0, tiled=True)
    return jnp.sum(tiles, axis=0)


def filled_up(lines, size):
    spare = -lines.shape[0] % size
    if not spare:
        return lines
    return jnp.concatenate([lines, jnp.zeros((spare, *lines.shape[1:]), lines.dtype)])


def joined_along(tiles, dim):
    lengths = list(tiles.shape[1:])
    lengths[dim] *= tiles.shape[0]
    return jnp.moveaxis(tiles, 0, dim).reshape(lengths)


def gather_directly(value, axis, dim):
    return joined_along(copy_for_each(value, axis), dim)


def sum_by_parts(value, axes):
    lines = value.reshape(-1, value.shape[-1])
    own = summed_on_arrival(filled_up(lines, lax.axis_size(axes)), axes, 0)
    whole = gather_directly(own, axes, 0)
    return whole[: len(lines)].reshape(value.shape)


def polar_steps(gram, width):
    highest = lax.Precision.HIGHEST
    scale = jnp.sqrt(jnp.sum(gram * gram) + 1e-06)
    ident = jnp.eye(width, dtype=jnp.float32)
    upper = gram / scale
    lower = ident
    for step in range(ITERS):
        middle = 0.5 * (3.0 * ident - jnp.dot(lower, upper, precision=highest))
        upper = jnp.dot(upper, middle, precision=highest)
        lower = jnp.dot(middle, lower, precision=highest)
    return (upper, lower, jnp.sqrt(scale))


def local(matrix, basis):
    highest = lax.Precision.HIGHEST
    width = basis.shape[1]
    nrow = lax.axis_size("row")
    ncol = lax.axis_size("col")
    partial_proj = lax.dot_general(
        lax.all_gather(basis, "col", axis=0, tiled=True),
        matrix,
        (((0,), (1,)), ((), ())),
        precision=highest,
    )
    proj = over_copies(partial_proj, "row")
    gram = sum_by_parts(jnp.dot(proj, proj.T, precision=highest), "col")
    upper, lower, root_scale = polar_steps(gram, width)
    right = jnp.dot(proj.T, lower, precision=highest) / root_scale
    root_full = upper * root_scale
    row_len = width // nrow
    col_len = width // ncol
    root = lax.dynamic_slice(
        root_full,
        (lax.axis_index("row") * row_len, lax.axis_index("col") * col_len),
        (row_len, col_len),
    )
    return (root, right)


def solution(mesh):
    return jax.shard_map(
        local,
        mesh=mesh,
        in_specs=(P("col", "row"), P(("row", "col"), None)),
        out_specs=(P("row", "col"), P("col", None)),
        check_vma=False,
    )
```

profile of v0, /device:TPU:32, one launch (start us, length us, event | category | flops | bytes accessed | tf_op | source)
XLA Modules:
  0.0 314.1 jit_solution(718308807394610721)
XLA Ops:
  7.2 0.0 copy-start
  7.2 0.0 all-gather.2.cloned.1.call-start
  7.2 0.7 all-gather.2.cloned.1.call-update
  7.9 143.3 %all-gather.2.cloned.1.call-done = f32[8192,512]{1,0:T(8,128)} async-done(((f32[256,512]{1,0:T(8,128)}), f32[8192,512]{1,0:T(8,128)}) %all-gather.2.cloned.1.call-update) | async-done | bytes 16777232 | tf_op jit(solution)/shard_map/all_gather | solution.py:72
  151.2 0.0 copy-done
  151.2 13.4 %fusion.11 = f32[512,64]{0,1:T(8,128)S(1)} fusion(f32[8192,512]{1,0:T(8,128)} %all-gather.2.cloned.1.call-done, f32[64,8192]{1,0:T(8,128)S(1)} %copy-done), kind=kOutput, calls=%fused_computation.24 | convolution fusion | flops 3221225472 | bytes 19005440 | tf_op jit(solution)/shard_map/dot_general | solution.py:71
  164.6 0.1 broadcast_in_dim.6
  164.7 20.0 %all_to_all.15 = f32[8,512,64]{1,2,0:T(8,128)S(1)} all-to-all(f32[8,512,64]{1,2,0:T(8,128)S(1)} %broadcast_in_dim.6), channel_id=1, replica_groups=mesh['row'=8,'col'=32] {'row'}, dimensions={0} | all-to-all | bytes 2097152 | tf_op jit(solution)/shard_map/all_to_all | solution.py:11
  184.8 0.1 reduce_sum.27
  184.8 0.1 copy.7
  185.0 1.0 fusion.9
  186.0 35.6 %all_to_all.16 = f32[32,16,512]{2,1,0:T(8,128)S(1)} all-to-all(f32[32,16,512]{2,1,0:T(8,128)S(1)} %fusion.9), channel_id=1, replica_groups=mesh['row'=8,'col'=32] {'col'}, dimensions={0} | all-to-all | bytes 2097152 | tf_op jit(solution)/shard_map/all_to_all | solution.py:25
  221.5 0.1 reduce_sum.28
  221.6 1.1 broadcast_in_dim.7
  222.7 5.7 %all-to-all-start.2 = ((f32[32,16,512]{2,1,0:T(8,128)}), f32[32,16,512]{2,1,0:T(8,128)S(1)}, u32[]{:S(2)}, u32[]{:S(2)}) async-start(f32[32,16,512]{2,1,0:T(8,128)} %broadcast_in_dim.7), calls=%async_computation.2 | async-start | bytes 2097152 | tf_op jit(solution)/shard_map/all_to_all | solution.py:11
  228.4 27.5 %all-to-all-done.2 = f32[32,16,512]{2,1,0:T(8,128)S(1)} async-done(((f32[32,16,512]{2,1,0:T(8,128)}), f32[32,16,512]{2,1,0:T(8,128)S(1)}, u32[]{:S(2)}, u32[]{:S(2)}) %all-to-all-start.2) | async-done | bytes 1048608 | tf_op jit(solution)/shard_map/all_to_all | solution.py:11
  255.9 0.9 multiply_reduce_fusion
  257.5 0.1 broadcast_divide_fusion
  257.6 1.1 fusion.7
  258.7 1.8 fusion.12
  260.6 1.0 fusion.8
  261.6 1.9 fusion
  263.4 1.8 fusion.13
  265.3 1.8 fusion.14
  267.1 1.8 fusion.1
  269.0 2.0 fusion.16
  271.0 1.8 fusion.15
  272.9 1.9 fusion.2
  274.7 1.8 fusion.18
  276.6 1.8 fusion.17
  278.4 1.8 fusion.3
  280.3 1.8 fusion.20
  282.2 2.1 fusion.19
  284.3 1.8 fusion.4
  286.1 1.8 fusion.22
  288.0 1.8 fusion.21
  289.8 1.8 fusion.5
  291.7 1.8 fusion.24
  293.5 2.8 fusion.23
  296.4 3.3 %fusion.6 = f32[512,512]{1,0:T(8,128)S(1)} fusion(f32[512,512]{1,0:T(8,128)S(1)} %fusion.24, f32[512,512]{1,0:T(8,128)} %fusion.23), kind=kOutput, calls=%fused_computation.14 | convolution fusion | flops 1611661312 | bytes 3145728 | tf_op jit(solution)/shard_map/dot_general | solution.py:60
  299.8 1.8 fusion.26
  301.6 3.1 fusion.25
  304.7 1.4 convolution_divide_fusion
  306.1 0.7 dynamic-slice_multiply_fusion
Async XLA Ops:
  7.2 144.0 %copy-start = (f32[64,8192]{1,0:T(8,128)S(1)}, f32[64,8192]{1,0:T(8,128)}, u32[]{:S(2)}) copy-start(f32[64,8192]{1,0:T(8,128)} %param.2) | copy-start | bytes 6291460
  7.2 144.0 %all-gather.2.cloned.1.call-start = ((), (), s32[]{:S(2)}) async-start(), calls=%async_computation.3 | async-start | bytes 17301504 | tf_op jit(solution)/shard_map/all_gather | solution.py:72
  222.7 33.2 %all-to-all-start.2 = ((f32[32,16,512]{2,1,0:T(8,128)}), f32[32,16,512]{2,1,0:T(8,128)S(1)}, u32[]{:S(2)}, u32[]{:S(2)}) async-start(f32[32,16,512]{2,1,0:T(8,128)} %broadcast_in_dim.7), calls=%async_computation.2 | async-start | bytes 2097152 | tf_op jit(solution)/shard_map/all_to_all | solution.py:11
Sparse Core Ops, SparseCore 0:
  10.6 140.5 all-gather.1
where the time goes:
time: 319 us; the launch traced here: 314 us
  waiting for transfers between devices  171 us (54%)
  matrix products  62.7 us (20%)
  blocking collectives  55.6 us (17%)
  between operations  15.5 us (5%)
  starting transfers between devices  5.7 us (2%)
    all_gather x1, waiting for transfers between devices, local(): lax.all_gather(basis, 'col', axis=0, tiled=True)  143 us
    all_to_all x1, blocking collectives, summed_on_arrival(): tiles = lax.all_to_all(cut_along(value, dim, size), axis, 0, 0, tiled=True)  35.6 us
    all_to_all x1, waiting for transfers between devices, copy_for_each(): return lax.all_to_all(copies, axis, split_axis=0, concat_axis=0, tiled=True)  27.5 us
    all_to_all x1, blocking collectives, copy_for_each(): return lax.all_to_all(copies, axis, split_axis=0, concat_axis=0, tiled=True)  20 us
    dot_general x8, matrix products, polar_steps(): upper = jnp.dot(upper, middle, precision=highest)  17.2 us
    dot_general x8, matrix products, polar_steps(): middle = 0.5 * (3.0 * ident - jnp.dot(lower, upper, precision=highest))  15.5 us
    dot_general x8, matrix products, polar_steps(): lower = jnp.dot(middle, lower, precision=highest)  14.1 us
    dot_general x1, matrix products, local(): lax.dot_general(lax.all_gather(basis, 'col', axis=0, tiled=True), matrix,...  13.4 us
  transfers between devices with their start and end apart: 2, of which 2 were waited for; matrix products, arithmetic and copies ran while one was open for 0% of the time, Pallas kernels for 0%

commit v1 on v0

v1 whole, which is shorter than its diff:
```python
import functools

import jax
import jax.numpy as jnp
from jax import lax
from jax.experimental import pallas as pl
from jax.experimental.pallas import tpu as pltpu
from jax.sharding import Mesh
from jax.sharding import PartitionSpec as P

ITERS = 8
HIGHEST = lax.Precision.HIGHEST


def shift(value, axis, by):
    size = lax.axis_size(axis)
    return lax.ppermute(value, axis, [(i, (i + by) % size) for i in range(size)])


def high_low(value):
    high = value.astype(jnp.bfloat16)
    return high, (value - high.astype(jnp.float32)).astype(jnp.bfloat16)


def dot3(left, right):
    (lh, ll), (rh, rl) = left, right
    dot = functools.partial(jnp.dot, preferred_element_type=jnp.float32)
    return dot(lh, rh) + (dot(lh, rl) + dot(ll, rh))


WHOLE = pl.BlockSpec(memory_space=pltpu.VMEM)
SCALARS = pl.BlockSpec(memory_space=pltpu.SMEM)


def column(where, offset, depth, count):
    return pl.multiple_of(lax.rem(where + (offset + count), count) * depth, depth)


def first_kernel(offsets, nz, at, q0, q1, q2, q3, own, *rest):
    pieces, (acc, high, low) = rest[:-3], rest[-3:]
    lines = q0.shape[0]
    for k, quarter in enumerate((q0, q1, q2, q3)):
        rows = pl.ds(pl.multiple_of(lax.rem(at[0] + k, 4) * lines, lines), lines)
        high[rows, :], low[rows, :] = high_low(quarter[...])
    depth = own.shape[0]
    cols = pl.ds(column(at[1], 0, depth, nz), depth)
    acc[...] = dot3((high[:, cols], low[:, cols]), high_low(own[...]))
    add_chunks(offsets, nz, at, high, low, pieces, acc)


def add_chunks(offsets, nz, at, high, low, pieces, acc):
    for i, offset in enumerate(offsets):
        chunk = jnp.concatenate([pieces[2 * i][...], pieces[2 * i + 1][...]], axis=0)
        depth = chunk.shape[0]
        cols = pl.ds(column(at[1], offset, depth, nz), depth)
        acc[...] += dot3((high[:, cols], low[:, cols]), high_low(chunk))


def middle_kernel(offsets, nz, at, high, low, before, *rest):
    pieces, acc = rest[:-1], rest[-1]
    acc[...] = before[...]
    add_chunks(offsets, nz, at, high, low, pieces, acc)


def last_kernel(offsets, nz, share, at, high, low, before, *rest):
    pieces, (keep, give, acc) = rest[:-3], rest[-3:]
    acc[...] = before[...]
    add_chunks(offsets, nz, at, high, low, pieces, acc)
    for i in range(keep.shape[0] // share):
        for core, out in ((at[2], keep), (1 - at[2], give)):
            rows = pl.ds(pl.multiple_of((2 * i + core) * share, share), share)
            out[i * share : (i + 1) * share, :] = acc[rows, :]


def cost(flops, size):
    return pl.CostEstimate(flops=flops, bytes_accessed=size, transcendentals=0)


def f32(*shape):
    return jax.ShapeDtypeStruct(shape, jnp.float32)


def bf16(*shape):
    return jax.ShapeDtypeStruct(shape, jnp.bfloat16)


def polar_kernel(row_ref, gram_ref, proj_ref, root_ref, right_ref, mh, ml, mf, xf):
    width = gram_ref.shape[0]
    height, lines = root_ref.shape[0], proj_ref.shape[0]
    gram = gram_ref[...]
    scale = jnp.sqrt(jnp.sum(gram * gram) + 1e-06)
    root_scale = jnp.sqrt(scale)
    upper = gram / scale
    mf[...] = upper
    mh[...], ml[...] = high_low(upper)
    mine = mf[pl.ds(pl.multiple_of(row_ref[0] * height, height), height), :]
    xf[:height, :] = mine
    xf[height:, :] = proj_ref[...]

    def advance():
        x = xf[...]
        xf[...] = 1.5 * x - 0.5 * dot3(high_low(x), (mh[...], ml[...]))

    def step(_, carry):
        m = (mh[...], ml[...])
        part = 1.5 * mf[...] - 0.5 * dot3(m, m)
        advance()
        new = 1.5 * part - 0.5 * dot3(high_low(part), m)
        mf[...] = new
        mh[...], ml[...] = high_low(new)
        return carry

    lax.fori_loop(0, ITERS - 1, step, 0)
    advance()
    root_ref[...] = xf[:height, :] * root_scale
    right_ref[...] = xf[height:, :] / root_scale


def polar(row, gram, proj, height):
    width = gram.shape[0]
    half = pltpu.VMEM((width, width), jnp.bfloat16)
    return pl.pallas_call(
        polar_kernel,
        out_shape=(f32(height, width), f32(*proj.shape)),
        in_specs=[SCALARS, WHOLE, WHOLE],
        out_specs=(WHOLE, WHOLE),
        scratch_shapes=[
            half,
            half,
            pltpu.VMEM((width, width), jnp.float32),
            pltpu.VMEM((height + proj.shape[0], width), jnp.float32),
        ],
        name="polar",
    )(row, gram, proj)


def local(matrix, basis):
    width = basis.shape[1]
    nx, nc, ny, nz = (lax.axis_size(a) for a in ("x", "core", "y", "z"))
    x, c, y, z = (lax.axis_index(a) for a in ("x", "core", "y", "z"))
    depth = basis.shape[0]
    nrow, ncol = nx * nc, ny * nz
    lines = matrix.shape[0]

    span = depth * nz

    def part(k):
        return lax.dynamic_slice(matrix, (0, lax.rem(y + k, ny) * span), (lines, span))

    half = depth // 2
    chunks = {}
    fwd = [basis[:half], basis[half:]]
    bwd = list(fwd)
    quarters = [part(0), None, None, None]
    for k in range(1, nz // 2 + 1):
        for piece in range(2):
            if k < nz // 2 or piece == 0:
                fwd[piece] = shift(fwd[piece], "z", 1)
            if k < nz // 2 or piece == 1:
                bwd[piece] = shift(bwd[piece], "z", -1)
        if k < nz // 2:
            chunks[-k], chunks[k] = tuple(fwd), tuple(bwd)
        else:
            chunks[k] = (fwd[0], bwd[1])
        if k < ny:
            quarters[-k % ny] = shift(part(k), "y", k)

    at = jnp.stack([y, z, c]).astype(jnp.int32)
    high = bf16(ny * lines, span)
    total = f32(ny * lines, width)
    each = 6 * ny * lines * depth * width

    def pieces_of(offsets):
        return [piece for k in offsets for piece in chunks[k]]

    offsets = (1, -1, 2, -2)
    acc, high, low = pl.pallas_call(
        functools.partial(first_kernel, offsets, nz),
        out_shape=(total, high, high),
        in_specs=[SCALARS] + [WHOLE] * (5 + 2 * len(offsets)),
        out_specs=(WHOLE,) * 3,
        cost_estimate=cost(5 * each, 8 << 20),
        name="first_chunks",
    )(at, *quarters, basis, *pieces_of(offsets))
    offsets = (3, -3)
    acc = pl.pallas_call(
        functools.partial(middle_kernel, offsets, nz),
        out_shape=total,
        in_specs=[SCALARS] + [WHOLE] * (3 + 2 * len(offsets)),
        out_specs=WHOLE,
        cost_estimate=cost(2 * each, 4 << 20),
        name="middle_chunks",
    )(at, high, low, acc, *pieces_of(offsets))
    offsets = (4,)
    share = lines // nrow
    keep, give = pl.pallas_call(
        functools.partial(last_kernel, offsets, nz, share),
        out_shape=(f32(ny * lines // nc, width),) * 2,
        in_specs=[SCALARS] + [WHOLE] * (3 + 2 * len(offsets)),
        out_specs=(WHOLE,) * 2,
        scratch_shapes=[pltpu.VMEM((ny * lines, width), jnp.float32)],
        cost_estimate=cost(each, 3 << 20),
        name="last_chunk",
    )(at, high, low, acc, *pieces_of(offsets))
    total = (keep + shift(give, "core", 1)).reshape(ny * nx, share, width)
    tiles = lax.all_to_all(total, ("y", "x"), 0, 0, tiled=True)
    own = tiles.sum(axis=0)
    copies = jnp.broadcast_to(own, (ny * nx, share, width))
    mine = lax.all_to_all(copies, ("y", "x"), 0, 0, tiled=True)
    other = shift(mine, "core", 1)
    even = jnp.where(c == 0, mine, other)
    odd = jnp.where(c == 0, other, mine)
    proj = jnp.stack([even, odd], axis=1).reshape(ny * lines, width)
    here = lax.dynamic_slice(proj, (y * lines, 0), (lines, width))
    tall = width // (ny * nrow)
    index = (y * nx + x) * nc + c
    some = lax.dynamic_slice(proj, (0, index * tall), (ny * lines, tall))
    gram = lax.dot_general(some, proj, (((0,), (0,)), ((), ())), precision=HIGHEST)
    copies = jnp.broadcast_to(gram, (nz, tall, width))
    gram = lax.all_to_all(copies, "z", 0, 0, tiled=True).sum(axis=0)
    copies = jnp.broadcast_to(gram, (ny * nx, tall, width))
    gram = lax.all_to_all(copies, ("y", "x"), 0, 0, tiled=True)
    other = shift(gram, "core", 1)
    even = jnp.where(c == 0, gram, other)
    odd = jnp.where(c == 0, other, gram)
    gram = jnp.stack([even, odd], axis=1).reshape(width, width)
    row = x * nc + c
    root, right = polar(row.reshape(1), gram, here, width // nrow)
    root = lax.dynamic_slice(root, (0, (y * nz + z) * (width // ncol)), (width // nrow, width // ncol))
    return (root, right)


def solution(mesh):
    fine = Mesh(mesh.devices.reshape(4, 2, 4, 8), ("x", "core", "y", "z"))
    return jax.shard_map(
        local,
        mesh=fine,
        in_specs=(P(("y", "z"), ("x", "core")), P(("x", "core", "y", "z"), None)),
        out_specs=(P(("x", "core"), ("y", "z")), P(("y", "z"), None)),
        check_vma=False,
    )
```

time: 319 us -> 155 us (0.49)
  the two profiles are of different devices: /device:TPU:32 before, /device:TPU:1 now
where the time goes in v1:
time: 155 us
  blocking collectives  54.1 us (35%)
  starting transfers between devices  46.7 us (30%)
  Pallas kernels  29.1 us (19%)
  waiting for transfers between devices  14.4 us (9%)
  local copies, waits for them, and re-layouts  6.62 us (4%)
  other arithmetic  2.93 us (2%)
    ppermute x20, starting transfers between devices, shift(): lax.ppermute(value, axis, [(i, (i + by) % size) for i in range(size)])  46.7 us
    pallas_call x1, Pallas kernels, polar(): pl.pallas_call(polar_kernel, out_shape=(f32(height, width), f32(*proj.sha...  17.7 us
    all_to_all x1, blocking collectives, local(): gram = lax.all_to_all(copies, 'z', 0, 0, tiled=True).sum(axis=0)  16.1 us
    all_to_all x1, blocking collectives, local(): tiles = lax.all_to_all(total, ('y', 'x'), 0, 0, tiled=True)  15.2 us
    ppermute x20, waiting for transfers between devices, shift(): lax.ppermute(value, axis, [(i, (i + by) % size) for i in range(size)])  14.4 us
    all_to_all x1, blocking collectives, local(): gram = lax.all_to_all(copies, ('y', 'x'), 0, 0, tiled=True)  12.4 us
    all_to_all x1, blocking collectives, local(): mine = lax.all_to_all(copies, ('y', 'x'), 0, 0, tiled=True)  10.4 us
    pallas_call x1, Pallas kernels, local(): pl.pallas_call(functools.partial(first_kernel, offsets, nz), out_shape=(t...  4.94 us
  transfers between devices with their start and end apart: 20, of which 11 were waited for; matrix products, arithmetic and copies ran while one was open for 2% of the time, Pallas kernels for 5%

profile of v1, /device:TPU:1, one launch (start us, length us, event | category | flops | bytes accessed | tf_op | source)
XLA Modules:
  0.0 155.1 jit_solution(15554305346382817228)
XLA Ops:
  0.6 1.1 fusion.3
  1.7 2.5 %collective-permute-start.6 = (f32[128,512]{1,0:T(8,128)S(1)}, f32[128,512]{1,0:T(8,128)S(1)}, u32[]{:S(2)}, u32[]{:S(2)}) collective-permute-start(f32[128,512]{1,0:T(8,128)S(1)} %get-tuple-element.28), channel_id=1, source_target_pairs={{0,1},{1,2},{2,3},{3,4},{4,5},{5,6},{6,7},{7,0},{8,9},{9,10},{10,1... | collective-permute-start | bytes 786440 | tf_op jit(solution)/shard_map/ppermute | solution.py:17
  4.2 2.5 %constant_dynamic-slice_fusion.2 = (f32[64,2048]{1,0:T(8,128)S(1)}, f32[64,2048]{1,0:T(8,128)S(1)}, f32[64,2048]{1,0:T(8,128)}, f32[64,2048]{1,0:T(8,128)S(1)}) fusion(f32[64,8192]{1,0:T(8,128)} %param.2, s32[]{:T(128)S(6)} %select_n.50, s32[]{:T(128)S(6)} %select_n.48, s32[]{:T(128)S(6)} %select_n.47, s32[]{:T(128)S(6)} %select_n.49), kind=kLoop, calls=%fused_computation.12 | loop fusion | bytes 4194320 | tf_op jit(solution)/shard_map/dynamic_slice | solution.py:148
  6.7 2.7 %collective-permute-start = (f32[64,2048]{1,0:T(8,128)S(1)}, f32[64,2048]{1,0:T(8,128)S(1)}, u32[]{:S(2)}, u32[]{:S(2)}) collective-permute-start(f32[64,2048]{1,0:T(8,128)S(1)} %get-tuple-element.21), channel_id=1, source_target_pairs={{0,24},{8,0},{16,8},{24,16},{1,25},{9,1},{17,9},{25,17},{2,26},{10... | collective-permute-start | bytes 1572872 | tf_op jit(solution)/shard_map/ppermute | solution.py:17
  9.5 0.3 collective-permute-start.1
  9.8 1.6 %collective-permute-start.5 = (f32[128,512]{1,0:T(8,128)S(1)}, f32[128,512]{1,0:T(8,128)S(1)}, u32[]{:S(2)}, u32[]{:S(2)}) collective-permute-start(f32[128,512]{1,0:T(8,128)S(1)} %get-tuple-element.29), channel_id=1, source_target_pairs={{0,1},{1,2},{2,3},{3,4},{4,5},{5,6},{6,7},{7,0},{8,9},{9,10},{10,1... | collective-permute-start | bytes 786440 | tf_op jit(solution)/shard_map/ppermute | solution.py:17
  11.5 2.4 %collective-permute-start.4 = (f32[128,512]{1,0:T(8,128)S(1)}, f32[128,512]{1,0:T(8,128)S(1)}, u32[]{:S(2)}, u32[]{:S(2)}) collective-permute-start(f32[128,512]{1,0:T(8,128)S(1)} %get-tuple-element.28), channel_id=1, source_target_pairs={{0,7},{1,0},{2,1},{3,2},{4,3},{5,4},{6,5},{7,6},{8,15},{9,8},{10,9... | collective-permute-start | bytes 786440 | tf_op jit(solution)/shard_map/ppermute | solution.py:17
  13.8 0.4 collective-permute-done.6.rest_3_
  14.2 1.2 collective-permute-start.3
  15.4 3.9 %collective-permute-done.5.rest_2_ = f32[128,512]{1,0:T(8,128)S(1)} collective-permute-done((f32[128,512]{1,0:T(8,128)S(1)}, f32[128,512]{1,0:T(8,128)S(1)}, u32[]{:S(2)}, u32[]{:S(2)}) %collective-permute-start.5) | collective-permute-done | bytes 262176 | tf_op jit(solution)/shard_map/ppermute | solution.py:17
  19.3 0.0 collective-permute-start.9
  19.3 0.0 collective-permute-done.4.rest_1_
  19.3 0.0 copy-start.5
  19.3 2.7 %collective-permute-start.8 = (f32[128,512]{1,0:T(8,128)S(1)}, f32[128,512]{1,0:T(8,128)S(1)}, u32[]{:S(2)}, u32[]{:S(2)}) collective-permute-start(f32[128,512]{1,0:T(8,128)S(1)} %collective-permute-done.4.rest_1_), channel_id=1, source_target_pairs={{0,7},{1,0},{2,1},{3,2},{4,3},{5,4},{6,5},{7,6},{8,15},{9,8},{10,9... | collective-permute-start | bytes 786440 | tf_op jit(solution)/shard_map/ppermute | solution.py:17
  21.9 1.9 %collective-permute-done.3.rest_0_ = f32[128,512]{1,0:T(8,128)S(1)} collective-permute-done((f32[128,512]{1,0:T(8,128)S(1)}, f32[128,512]{1,0:T(8,128)S(1)}, u32[]{:S(2)}, u32[]{:S(2)}) %collective-permute-start.3) | collective-permute-done | bytes 262176 | tf_op jit(solution)/shard_map/ppermute | solution.py:17
  23.9 0.7 collective-permute-start.2
  24.5 0.0 collective-permute-done.q1
  24.6 3.4 %collective-permute-start.7 = (f32[128,512]{1,0:T(8,128)S(1)}, f32[128,512]{1,0:T(8,128)}, u32[]{:S(2)}, u32[]{:S(2)}) collective-permute-start(f32[128,512]{1,0:T(8,128)S(1)} %collective-permute-done.3.rest_0_), channel_id=1, source_target_pairs={{0,7},{1,0},{2,1},{3,2},{4,3},{5,4},{6,5},{7,6},{8,15},{9,8},{10,9... | collective-permute-start | bytes 786440 | tf_op jit(solution)/shard_map/ppermute | solution.py:17
  28.0 0.0 collective-permute-done.1.q2
  28.0 0.0 collective-permute-start.10
  28.0 0.0 collective-permute-done.9.rest_6_
  28.0 0.0 copy-start.7
  28.0 0.6 collective-permute-start.13
  28.6 0.9 collective-permute-done.8.rest_5_
  29.5 3.4 %collective-permute-start.12 = (f32[128,512]{1,0:T(8,128)S(1)}, f32[128,512]{1,0:T(8,128)}, u32[]{:S(2)}, u32[]{:S(2)}) collective-permute-start(f32[128,512]{1,0:T(8,128)S(1)} %collective-permute-done.8.rest_5_), channel_id=1, source_target_pairs={{0,7},{1,0},{2,1},{3,2},{4,3},{5,4},{6,5},{7,6},{8,15},{9,8},{10,9... | collective-permute-start | bytes 786440 | tf_op jit(solution)/shard_map/ppermute | solution.py:17
  32.9 1.1 collective-permute-done.7.rest_4_
  34.0 3.4 %collective-permute-start.11 = (f32[128,512]{1,0:T(8,128)}, f32[128,512]{1,0:T(8,128)}, u32[]{:S(2)}, u32[]{:S(2)}) collective-permute-start(f32[128,512]{1,0:T(8,128)} %collective-permute-done.7.rest_4_), channel_id=1, source_target_pairs={{0,7},{1,0},{2,1},{3,2},{4,3},{5,4},{6,5},{7,6},{8,15},{9,8},{10,9... | collective-permute-start | bytes 786440 | tf_op jit(solution)/shard_map/ppermute | solution.py:17
  37.4 0.0 collective-permute-done.10.rest_7_
  37.4 0.0 collective-permute-start.14
  37.4 0.1 collective-permute-done.13.rest_2_
  37.5 0.0 copy-done.8
  37.5 0.8 collective-permute-start.15
  38.3 0.0 collective-permute-done.12.rest_1_
  38.3 2.0 %collective-permute-start.16 = (f32[128,512]{1,0:T(8,128)}, f32[128,512]{1,0:T(8,128)}, u32[]{:S(2)}, u32[]{:S(2)}) collective-permute-start(f32[128,512]{1,0:T(8,128)} %collective-permute-done.12.rest_1_), channel_id=1, source_target_pairs={{0,7},{1,0},{2,1},{3,2},{4,3},{5,4},{6,5},{7,6},{8,15},{9,8},{10,9... | collective-permute-start | bytes 786440 | tf_op jit(solution)/shard_map/ppermute | solution.py:17
  40.4 0.6 pad_add_fusion.at
  41.0 0.0 collective-permute-done.2.q3
  41.0 0.0 copy-done.3
  41.0 0.8 copy-done.2
  41.8 4.9 %first_chunks.1 = (f32[256,512]{1,0:T(8,128)}, bf16[256,2048]{1,0:T(8,128)(2,1)}, bf16[256,2048]{1,0:T(8,128)(2,1)}) custom-call(s32[3]{0:T(128)} %pad_add_fusion.at, f32[64,2048]{1,0:T(8,128)} %get-tuple-element.22.q0, f32[64,2048]{1,0:T(8,128)} %copy-done, f32[64,2048]{1,0:T(8,128)} %copy-done.1, f32[64,2048]{1,0:T(8,128)} %copy-done.2, f32[256,512]{1,0:T(8,128)} %own.1, ...), custom_call_target="tpu_custom_call" | custom-call | flops 1006632960 | bytes 8388608 | tf_op jit(solution)/shard_map/first_chunks/pallas_call | solution.py:177
  46.7 0.0 collective-permute-done.11.rest_0_
  46.7 0.5 collective-permute-done.14.rest_3_
  47.2 3.4 %middle_chunks.1.before = f32[256,512]{1,0:T(8,128)} custom-call(s32[3]{0:T(128)} %pad_add_fusion.at, bf16[256,2048]{1,0:T(8,128)(2,1)} %get-tuple-element.9.high, bf16[256,2048]{1,0:T(8,128)(2,1)} %get-tuple-element.10.low, f32[256,512]{1,0:T(8,128)} %get-tuple-element.11.before, f32[128,512]{1,0:T(8,128)} %collective-permute-done.11.rest_0_, ...), custom_call_target="tpu_custom_call" | custom-call | flops 402653184 | bytes 4194304 | tf_op jit(solution)/shard_map/middle_chunks/pallas_call | solution.py:186
  50.6 2.2 %collective-permute-done.15.rest_0_ = f32[128,512]{1,0:T(8,128)} collective-permute-done((f32[128,512]{1,0:T(8,128)}, f32[128,512]{1,0:T(8,128)}, u32[]{:S(2)}, u32[]{:S(2)}) %collective-permute-start.15) | collective-permute-done | bytes 262176 | tf_op jit(solution)/shard_map/ppermute | solution.py:17
  52.9 0.0 collective-permute-done.16.rest_1_
  52.9 3.0 %last_chunk.1 = (f32[128,512]{1,0:T(8,128)}, f32[128,512]{1,0:T(8,128)}) custom-call(s32[3]{0:T(128)} %pad_add_fusion.at, bf16[256,2048]{1,0:T(8,128)(2,1)} %get-tuple-element.9.high, bf16[256,2048]{1,0:T(8,128)(2,1)} %get-tuple-element.10.low, f32[256,512]{1,0:T(8,128)} %middle_chunks.1.before, f32[128,512]{1,0:T(8,128)} %collective-permute-done.15.rest_0_, ...), custom_call_target="tpu_custom_call" | custom-call | flops 201326592 | bytes 3145728 | tf_op jit(solution)/shard_map/last_chunk/pallas_call | solution.py:196
  55.9 13.4 %collective-permute-start.17 = (f32[128,512]{1,0:T(8,128)}, f32[128,512]{1,0:T(8,128)S(1)}, u32[]{:S(2)}, u32[]{:S(2)}) collective-permute-start(f32[128,512]{1,0:T(8,128)} %get-tuple-element.13), channel_id=1, source_target_pairs={{0,32},{32,0},{1,33},{33,1},{2,34},{34,2},{3,35},{35,3},{4,36},{36... | collective-permute-start | bytes 786440 | tf_op jit(solution)/shard_map/ppermute | solution.py:17
  69.3 1.4 collective-permute-done.17
  70.7 1.0 add_bitcast_fusion
  71.6 15.2 %all_to_all.20 = f32[16,8,512]{2,1,0:T(8,128)S(1)} all-to-all(f32[16,8,512]{2,1,0:T(8,128)S(1)} %add_bitcast_fusion), channel_id=1, replica_groups=mesh['x'=4,'core'=2,'y'=4,'z'=8] {'y','x'}, dimensions={0} | all-to-all | bytes 524288 | tf_op jit(solution)/shard_map/all_to_all | solution.py:206
  86.9 10.4 %all_to_all.21 = f32[16,8,512]{2,1,0:T(8,128)S(1)} all-to-all(f32[16,8,512]{2,1,0:T(8,128)S(1)} %broadcast_in_dim.9), channel_id=1, replica_groups=mesh['x'=4,'core'=2,'y'=4,'z'=8] {'y','x'}, dimensions={0} | all-to-all | bytes 524288 | tf_op jit(solution)/shard_map/all_to_all | solution.py:209
  97.3 2.7 %collective-permute-start.18 = (f32[16,8,512]{2,1,0:T(8,128)S(1)}, f32[16,8,512]{2,1,0:T(8,128)S(1)}, u32[]{:S(2)}, u32[]{:S(2)}) collective-permute-start(f32[16,8,512]{2,1,0:T(8,128)S(1)} %all_to_all.21), channel_id=1, source_target_pairs={{0,32},{32,0},{1,33},{33,1},{2,34},{34,2},{3,35},{35,3},{4,36},{36... | collective-permute-start | bytes 786440 | tf_op jit(solution)/shard_map/ppermute | solution.py:17
  100.0 1.2 collective-permute-done.18
  101.3 0.4 fusion
  101.7 16.1 %all_to_all.22 = f32[8,16,512]{2,1,0:T(8,128)S(1)} all-to-all(f32[8,16,512]{2,1,0:T(8,128)S(1)} %broadcast_in_dim.10), channel_id=1, replica_groups=mesh['x'=4,'core'=2,'y'=4,'z'=8] {'z'}, dimensions={0} | all-to-all | bytes 524288 | tf_op jit(solution)/shard_map/all_to_all | solution.py:220
  117.9 0.1 broadcast_in_dim.11
  117.9 12.4 %all_to_all.23 = f32[16,16,512]{2,1,0:T(8,128)S(1)} all-to-all(f32[16,16,512]{2,1,0:T(8,128)S(1)} %broadcast_in_dim.11), channel_id=1, replica_groups=mesh['x'=4,'core'=2,'y'=4,'z'=8] {'y','x'}, dimensions={0} | all-to-all | bytes 1048576 | tf_op jit(solution)/shard_map/all_to_all | solution.py:222
  130.3 2.8 %collective-permute-start.19 = (f32[16,16,512]{2,1,0:T(8,128)S(1)}, f32[16,16,512]{2,1,0:T(8,128)S(1)}, u32[]{:S(2)}, u32[]{:S(2)}) collective-permute-start(f32[16,16,512]{2,1,0:T(8,128)S(1)} %all_to_all.23), channel_id=1, source_target_pairs={{0,32},{32,0},{1,33},{33,1},{2,34},{34,2},{3,35},{35,3},{4,36},{36... | collective-permute-start | bytes 1572872 | tf_op jit(solution)/shard_map/ppermute | solution.py:17
  133.1 0.7 constant_dynamic-slice_fusion.1.proj_ref
  133.8 0.9 collective-permute-done.19
  134.6 0.1 select_bitcast_fusion.1
  134.8 1.1 pad_maximum_fusion
  135.9 17.7 %polar.1 = (f32[64,512]{1,0:T(8,128)}, f32[64,512]{1,0:T(8,128)}) custom-call(s32[1]{0:T(128)} %bitcast.row_ref, f32[512,512]{1,0:T(8,128)} %bitcast.21, f32[64,512]{1,0:T(8,128)} %constant_dynamic-slice_fusion.1.proj_ref), custom_call_target="tpu_custom_call" | custom-call | tf_op jit(solution)/shard_map/polar/pallas_call | solution.py:122
  153.6 0.8 constant_dynamic-slice_fusion
  154.4 0.7 copy.9
  (19 shorter events, 0.2 us)
Async XLA Ops:
  1.7 12.5 %collective-permute-start.6 = (f32[128,512]{1,0:T(8,128)S(1)}, f32[128,512]{1,0:T(8,128)S(1)}, u32[]{:S(2)}, u32[]{:S(2)}) collective-permute-start(f32[128,512]{1,0:T(8,128)S(1)} %get-tuple-element.28), channel_id=1, source_target_pairs={{0,1},{1,2},{2,3},{3,4},{4,5},{5,6},{6,7},{7,0},{8,9},{9,10},{10,1... | collective-permute-start | bytes 786440 | tf_op jit(solution)/shard_map/ppermute | solution.py:17
  6.7 17.8 %collective-permute-start = (f32[64,2048]{1,0:T(8,128)S(1)}, f32[64,2048]{1,0:T(8,128)S(1)}, u32[]{:S(2)}, u32[]{:S(2)}) collective-permute-start(f32[64,2048]{1,0:T(8,128)S(1)} %get-tuple-element.21), channel_id=1, source_target_pairs={{0,24},{8,0},{16,8},{24,16},{1,25},{9,1},{17,9},{25,17},{2,26},{10... | collective-permute-start | bytes 1572872 | tf_op jit(solution)/shard_map/ppermute | solution.py:17
  9.5 18.5 %collective-permute-start.1 = (f32[64,2048]{1,0:T(8,128)S(1)}, f32[64,2048]{1,0:T(8,128)S(1)}, u32[]{:S(2)}, u32[]{:S(2)}) collective-permute-start(f32[64,2048]{1,0:T(8,128)S(1)} %get-tuple-element.23), channel_id=1, source_target_pairs={{0,16},{8,24},{16,0},{24,8},{1,17},{9,25},{17,1},{25,9},{2,18},{10... | collective-permute-start | bytes 1572872 | tf_op jit(solution)/shard_map/ppermute | solution.py:17
  9.8 9.4 %collective-permute-start.5 = (f32[128,512]{1,0:T(8,128)S(1)}, f32[128,512]{1,0:T(8,128)S(1)}, u32[]{:S(2)}, u32[]{:S(2)}) collective-permute-start(f32[128,512]{1,0:T(8,128)S(1)} %get-tuple-element.29), channel_id=1, source_target_pairs={{0,1},{1,2},{2,3},{3,4},{4,5},{5,6},{6,7},{7,0},{8,9},{9,10},{10,1... | collective-permute-start | bytes 786440 | tf_op jit(solution)/shard_map/ppermute | solution.py:17
  11.5 7.8 %collective-permute-start.4 = (f32[128,512]{1,0:T(8,128)S(1)}, f32[128,512]{1,0:T(8,128)S(1)}, u32[]{:S(2)}, u32[]{:S(2)}) collective-permute-start(f32[128,512]{1,0:T(8,128)S(1)} %get-tuple-element.28), channel_id=1, source_target_pairs={{0,7},{1,0},{2,1},{3,2},{4,3},{5,4},{6,5},{7,6},{8,15},{9,8},{10,9... | collective-permute-start | bytes 786440 | tf_op jit(solution)/shard_map/ppermute | solution.py:17
  14.2 26.8 %copy-start.3 = (f32[128,512]{1,0:T(8,128)}, f32[128,512]{1,0:T(8,128)S(1)}, u32[]{:S(2)}) copy-start(f32[128,512]{1,0:T(8,128)S(1)} %collective-permute-done.6.rest_3_) | copy-start | bytes 786436
  14.2 9.7 %collective-permute-start.3 = (f32[128,512]{1,0:T(8,128)S(1)}, f32[128,512]{1,0:T(8,128)S(1)}, u32[]{:S(2)}, u32[]{:S(2)}) collective-permute-start(f32[128,512]{1,0:T(8,128)S(1)} %get-tuple-element.29), channel_id=1, source_target_pairs={{0,7},{1,0},{2,1},{3,2},{4,3},{5,4},{6,5},{7,6},{8,15},{9,8},{10,9... | collective-permute-start | bytes 786440 | tf_op jit(solution)/shard_map/ppermute | solution.py:17
  19.3 21.7 %copy-start.4 = (f32[128,512]{1,0:T(8,128)}, f32[128,512]{1,0:T(8,128)S(1)}, u32[]{:S(2)}) copy-start(f32[128,512]{1,0:T(8,128)S(1)} %collective-permute-done.5.rest_2_) | copy-start | bytes 786436
  19.3 8.7 %collective-permute-start.9 = (f32[128,512]{1,0:T(8,128)S(1)}, f32[128,512]{1,0:T(8,128)S(1)}, u32[]{:S(2)}, u32[]{:S(2)}) collective-permute-start(f32[128,512]{1,0:T(8,128)S(1)} %collective-permute-done.5.rest_2_), channel_id=1, source_target_pairs={{0,1},{1,2},{2,3},{3,4},{4,5},{5,6},{6,7},{7,0},{8,9},{9,10},{10,1... | collective-permute-start | bytes 786440 | tf_op jit(solution)/shard_map/ppermute | solution.py:17
  19.3 21.7 %copy-start.5 = (f32[128,512]{1,0:T(8,128)}, f32[128,512]{1,0:T(8,128)S(1)}, u32[]{:S(2)}) copy-start(f32[128,512]{1,0:T(8,128)S(1)} %collective-permute-done.4.rest_1_) | copy-start | bytes 786436
  19.3 10.2 %collective-permute-start.8 = (f32[128,512]{1,0:T(8,128)S(1)}, f32[128,512]{1,0:T(8,128)S(1)}, u32[]{:S(2)}, u32[]{:S(2)}) collective-permute-start(f32[128,512]{1,0:T(8,128)S(1)} %collective-permute-done.4.rest_1_), channel_id=1, source_target_pairs={{0,7},{1,0},{2,1},{3,2},{4,3},{5,4},{6,5},{7,6},{8,15},{9,8},{10,9... | collective-permute-start | bytes 786440 | tf_op jit(solution)/shard_map/ppermute | solution.py:17
  23.9 17.1 %copy-start.6 = (f32[128,512]{1,0:T(8,128)}, f32[128,512]{1,0:T(8,128)S(1)}, u32[]{:S(2)}) copy-start(f32[128,512]{1,0:T(8,128)S(1)} %collective-permute-done.3.rest_0_) | copy-start | bytes 786436
  23.9 17.1 %collective-permute-start.2 = (f32[64,2048]{1,0:T(8,128)S(1)}, f32[64,2048]{1,0:T(8,128)S(1)}, u32[]{:S(2)}, u32[]{:S(2)}) collective-permute-start(f32[64,2048]{1,0:T(8,128)S(1)} %get-tuple-element.20), channel_id=1, source_target_pairs={{0,8},{8,16},{16,24},{24,0},{1,9},{9,17},{17,25},{25,1},{2,10},{10... | collective-permute-start | bytes 1572872 | tf_op jit(solution)/shard_map/ppermute | solution.py:17
  24.6 16.5 %copy-start = (f32[64,2048]{1,0:T(8,128)}, f32[64,2048]{1,0:T(8,128)S(1)}, u32[]{:S(2)}) copy-start(f32[64,2048]{1,0:T(8,128)S(1)} %collective-permute-done.q1) | copy-start | bytes 1572868
  24.6 9.4 %collective-permute-start.7 = (f32[128,512]{1,0:T(8,128)S(1)}, f32[128,512]{1,0:T(8,128)}, u32[]{:S(2)}, u32[]{:S(2)}) collective-permute-start(f32[128,512]{1,0:T(8,128)S(1)} %collective-permute-done.3.rest_0_), channel_id=1, source_target_pairs={{0,7},{1,0},{2,1},{3,2},{4,3},{5,4},{6,5},{7,6},{8,15},{9,8},{10,9... | collective-permute-start | bytes 786440 | tf_op jit(solution)/shard_map/ppermute | solution.py:17
  28.0 13.0 %copy-start.1 = (f32[64,2048]{1,0:T(8,128)}, f32[64,2048]{1,0:T(8,128)S(1)}, u32[]{:S(2)}) copy-start(f32[64,2048]{1,0:T(8,128)S(1)} %collective-permute-done.1.q2) | copy-start | bytes 1572868
  28.0 9.4 %collective-permute-start.10 = (f32[128,512]{1,0:T(8,128)S(1)}, f32[128,512]{1,0:T(8,128)}, u32[]{:S(2)}, u32[]{:S(2)}) collective-permute-start(f32[128,512]{1,0:T(8,128)S(1)} %collective-permute-done.6.rest_3_), channel_id=1, source_target_pairs={{0,1},{1,2},{2,3},{3,4},{4,5},{5,6},{6,7},{7,0},{8,9},{9,10},{10,1... | collective-permute-start | bytes 786440 | tf_op jit(solution)/shard_map/ppermute | solution.py:17
  28.0 13.0 %copy-start.7 = (f32[128,512]{1,0:T(8,128)}, f32[128,512]{1,0:T(8,128)S(1)}, u32[]{:S(2)}) copy-start(f32[128,512]{1,0:T(8,128)S(1)} %collective-permute-done.9.rest_6_) | copy-start | bytes 786436
  28.0 9.5 %collective-permute-start.13 = (f32[128,512]{1,0:T(8,128)S(1)}, f32[128,512]{1,0:T(8,128)}, u32[]{:S(2)}, u32[]{:S(2)}) collective-permute-start(f32[128,512]{1,0:T(8,128)S(1)} %collective-permute-done.9.rest_6_), channel_id=1, source_target_pairs={{0,1},{1,2},{2,3},{3,4},{4,5},{5,6},{6,7},{7,0},{8,9},{9,10},{10,1... | collective-permute-start | bytes 786440 | tf_op jit(solution)/shard_map/ppermute | solution.py:17
  29.5 8.0 %copy-start.8 = (f32[128,512]{1,0:T(8,128)}, f32[128,512]{1,0:T(8,128)S(1)}, u32[]{:S(2)}) copy-start(f32[128,512]{1,0:T(8,128)S(1)} %collective-permute-done.8.rest_5_) | copy-start | bytes 786436
  29.5 8.9 %collective-permute-start.12 = (f32[128,512]{1,0:T(8,128)S(1)}, f32[128,512]{1,0:T(8,128)}, u32[]{:S(2)}, u32[]{:S(2)}) collective-permute-start(f32[128,512]{1,0:T(8,128)S(1)} %collective-permute-done.8.rest_5_), channel_id=1, source_target_pairs={{0,7},{1,0},{2,1},{3,2},{4,3},{5,4},{6,5},{7,6},{8,15},{9,8},{10,9... | collective-permute-start | bytes 786440 | tf_op jit(solution)/shard_map/ppermute | solution.py:17
  34.0 12.7 %collective-permute-start.11 = (f32[128,512]{1,0:T(8,128)}, f32[128,512]{1,0:T(8,128)}, u32[]{:S(2)}, u32[]{:S(2)}) collective-permute-start(f32[128,512]{1,0:T(8,128)} %collective-permute-done.7.rest_4_), channel_id=1, source_target_pairs={{0,7},{1,0},{2,1},{3,2},{4,3},{5,4},{6,5},{7,6},{8,15},{9,8},{10,9... | collective-permute-start | bytes 786440 | tf_op jit(solution)/shard_map/ppermute | solution.py:17
  37.4 9.9 %collective-permute-start.14 = (f32[128,512]{1,0:T(8,128)}, f32[128,512]{1,0:T(8,128)}, u32[]{:S(2)}, u32[]{:S(2)}) collective-permute-start(f32[128,512]{1,0:T(8,128)} %collective-permute-done.10.rest_7_), channel_id=1, source_target_pairs={{0,1},{1,2},{2,3},{3,4},{4,5},{5,6},{6,7},{7,0},{8,9},{9,10},{10,1... | collective-permute-start | bytes 786440 | tf_op jit(solution)/shard_map/ppermute | solution.py:17
  37.5 15.4 %collective-permute-start.15 = (f32[128,512]{1,0:T(8,128)}, f32[128,512]{1,0:T(8,128)}, u32[]{:S(2)}, u32[]{:S(2)}) collective-permute-start(f32[128,512]{1,0:T(8,128)} %collective-permute-done.13.rest_2_), channel_id=1, source_target_pairs={{0,1},{1,2},{2,3},{3,4},{4,5},{5,6},{6,7},{7,0},{8,9},{9,10},{10,1... | collective-permute-start | bytes 786440 | tf_op jit(solution)/shard_map/ppermute | solution.py:17
  38.3 14.5 %collective-permute-start.16 = (f32[128,512]{1,0:T(8,128)}, f32[128,512]{1,0:T(8,128)}, u32[]{:S(2)}, u32[]{:S(2)}) collective-permute-start(f32[128,512]{1,0:T(8,128)} %collective-permute-done.12.rest_1_), channel_id=1, source_target_pairs={{0,7},{1,0},{2,1},{3,2},{4,3},{5,4},{6,5},{7,6},{8,15},{9,8},{10,9... | collective-permute-start | bytes 786440 | tf_op jit(solution)/shard_map/ppermute | solution.py:17
  41.0 0.8 copy-start.2
  55.9 14.8 %collective-permute-start.17 = (f32[128,512]{1,0:T(8,128)}, f32[128,512]{1,0:T(8,128)S(1)}, u32[]{:S(2)}, u32[]{:S(2)}) collective-permute-start(f32[128,512]{1,0:T(8,128)} %get-tuple-element.13), channel_id=1, source_target_pairs={{0,32},{32,0},{1,33},{33,1},{2,34},{34,2},{3,35},{35,3},{4,36},{36... | collective-permute-start | bytes 786440 | tf_op jit(solution)/shard_map/ppermute | solution.py:17
  97.3 3.9 %collective-permute-start.18 = (f32[16,8,512]{2,1,0:T(8,128)S(1)}, f32[16,8,512]{2,1,0:T(8,128)S(1)}, u32[]{:S(2)}, u32[]{:S(2)}) collective-permute-start(f32[16,8,512]{2,1,0:T(8,128)S(1)} %all_to_all.21), channel_id=1, source_target_pairs={{0,32},{32,0},{1,33},{33,1},{2,34},{34,2},{3,35},{35,3},{4,36},{36... | collective-permute-start | bytes 786440 | tf_op jit(solution)/shard_map/ppermute | solution.py:17
  130.3 4.3 %collective-permute-start.19 = (f32[16,16,512]{2,1,0:T(8,128)S(1)}, f32[16,16,512]{2,1,0:T(8,128)S(1)}, u32[]{:S(2)}, u32[]{:S(2)}) collective-permute-start(f32[16,16,512]{2,1,0:T(8,128)S(1)} %all_to_all.23), channel_id=1, source_target_pairs={{0,32},{32,0},{1,33},{33,1},{2,34},{34,2},{3,35},{35,3},{4,36},{36... | collective-permute-start | bytes 1572872 | tf_op jit(solution)/shard_map/ppermute | solution.py:17

commit v2 on v1

--- a/solution.py
+++ b/solution.py
@@ -72,6 +72,9 @@
             out[i * share : (i + 1) * share, :] = acc[rows, :]
 
 
+PARAMS = pltpu.CompilerParams(vmem_limit_bytes=24 << 20)
+
+
 def cost(flops, size):
     return pl.CostEstimate(flops=flops, bytes_accessed=size, transcendentals=0)
 
@@ -84,18 +87,26 @@
     return jax.ShapeDtypeStruct(shape, jnp.bfloat16)
 
 
-def polar_kernel(row_ref, gram_ref, proj_ref, root_ref, right_ref, mh, ml, mf, xf):
-    width = gram_ref.shape[0]
-    height, lines = root_ref.shape[0], proj_ref.shape[0]
-    gram = gram_ref[...]
+def polar_kernel(at, mine_ref, other_ref, here_ref, there_ref, root_ref, right_ref, mh, ml, mf, xf):
+    width = mf.shape[0]
+    short, height = root_ref.shape
+    chips, tall, _ = mine_ref.shape
+    groups, share, _ = here_ref.shape
+    for chip in range(chips):
+        for core, ref in ((at[1], mine_ref), (1 - at[1], other_ref)):
+            rows = pl.ds(pl.multiple_of((2 * chip + core) * tall, tall), tall)
+            mf[rows, :] = ref[chip]
+    gram = mf[...]
     scale = jnp.sqrt(jnp.sum(gram * gram) + 1e-06)
     root_scale = jnp.sqrt(scale)
     upper = gram / scale
     mf[...] = upper
     mh[...], ml[...] = high_low(upper)
-    mine = mf[pl.ds(pl.multiple_of(row_ref[0] * height, height), height), :]
-    xf[:height, :] = mine
-    xf[height:, :] = proj_ref[...]
+    xf[:short, :] = mf[pl.ds(pl.multiple_of(at[2] * short, short), short), :]
+    for group in range(groups):
+        for core, ref in ((at[1], here_ref), (1 - at[1], there_ref)):
+            row = short + (2 * group + core) * share
+            xf[pl.ds(pl.multiple_of(row, share), share), :] = ref[group]
 
     def advance():
         x = xf[...]
@@ -112,26 +123,31 @@
 
     lax.fori_loop(0, ITERS - 1, step, 0)
     advance()
-    root_ref[...] = xf[:height, :] * root_scale
-    right_ref[...] = xf[height:, :] / root_scale
-
-
-def polar(row, gram, proj, height):
-    width = gram.shape[0]
+    turned = pltpu.roll(xf[:short, :] * root_scale, lax.rem(width - at[0] * height, width), 1)
+    root_ref[...] = turned[:, :height]
+    right_ref[...] = xf[short:, :] / root_scale
+
+
+def polar(at, mine, other, here, there, root):
+    width = here.shape[2]
+    lines = 2 * here.shape[0] * here.shape[1]
+    height, short = root
     half = pltpu.VMEM((width, width), jnp.bfloat16)
-    return pl.pallas_call(
+    turned, right = pl.pallas_call(
         polar_kernel,
-        out_shape=(f32(height, width), f32(*proj.shape)),
-        in_specs=[SCALARS, WHOLE, WHOLE],
+        out_shape=(f32(short, height), f32(lines, width)),
+        in_specs=[SCALARS] + [WHOLE] * 4,
         out_specs=(WHOLE, WHOLE),
         scratch_shapes=[
             half,
             half,
             pltpu.VMEM((width, width), jnp.float32),
-            pltpu.VMEM((height + proj.shape[0], width), jnp.float32),
+            pltpu.VMEM((short + lines, width), jnp.float32),
         ],
+        compiler_params=PARAMS,
         name="polar",
-    )(row, gram, proj)
+    )(at, mine, other, here, there)
+    return (turned.T, right)
 
 
 def local(matrix, basis):
@@ -144,14 +160,15 @@
 
     span = depth * nz
 
-    def part(k):
-        return lax.dynamic_slice(matrix, (0, lax.rem(y + k, ny) * span), (lines, span))
+    def part(k, after=None):
+        whole = matrix if after is None else lax.optimization_barrier((matrix, after))[0]
+        return lax.dynamic_slice(whole, (0, lax.rem(y + k, ny) * span), (lines, span))
 
     half = depth // 2
     chunks = {}
     fwd = [basis[:half], basis[half:]]
     bwd = list(fwd)
-    quarters = [part(0), None, None, None]
+    quarters = [None] * ny
     for k in range(1, nz // 2 + 1):
         for piece in range(2):
             if k < nz // 2 or piece == 0:
@@ -162,8 +179,11 @@
             chunks[-k], chunks[k] = tuple(fwd), tuple(bwd)
         else:
             chunks[k] = (fwd[0], bwd[1])
-        if k < ny:
-            quarters[-k % ny] = shift(part(k), "y", k)
+        if k == 1:
+            for j, after in ((1, fwd[0]), (3, bwd[0]), (2, fwd[1])):
+                quarters[-j % ny] = shift(part(j, after), "y", j)
+        if k == 2:
+            quarters[0] = part(0, fwd[0])
 
     at = jnp.stack([y, z, c]).astype(jnp.int32)
     high = bf16(ny * lines, span)
@@ -180,6 +200,7 @@
         in_specs=[SCALARS] + [WHOLE] * (5 + 2 * len(offsets)),
         out_specs=(WHOLE,) * 3,
         cost_estimate=cost(5 * each, 8 << 20),
+        compiler_params=PARAMS,
         name="first_chunks",
     )(at, *quarters, basis, *pieces_of(offsets))
     offsets = (3, -3)
@@ -189,6 +210,7 @@
         in_specs=[SCALARS] + [WHOLE] * (3 + 2 * len(offsets)),
         out_specs=WHOLE,
         cost_estimate=cost(2 * each, 4 << 20),
+        compiler_params=PARAMS,
         name="middle_chunks",
     )(at, high, low, acc, *pieces_of(offsets))
     offsets = (4,)
@@ -200,34 +222,32 @@
         out_specs=(WHOLE,) * 2,
         scratch_shapes=[pltpu.VMEM((ny * lines, width), jnp.float32)],
         cost_estimate=cost(each, 3 << 20),
+        compiler_params=PARAMS,
         name="last_chunk",
     )(at, high, low, acc, *pieces_of(offsets))
     total = (keep + shift(give, "core", 1)).reshape(ny * nx, share, width)
     tiles = lax.all_to_all(total, ("y", "x"), 0, 0, tiled=True)
     own = tiles.sum(axis=0)
-    copies = jnp.broadcast_to(own, (ny * nx, share, width))
-    mine = lax.all_to_all(copies, ("y", "x"), 0, 0, tiled=True)
-    other = shift(mine, "core", 1)
-    even = jnp.where(c == 0, mine, other)
-    odd = jnp.where(c == 0, other, mine)
-    proj = jnp.stack([even, odd], axis=1).reshape(ny * lines, width)
-    here = lax.dynamic_slice(proj, (y * lines, 0), (lines, width))
-    tall = width // (ny * nrow)
-    index = (y * nx + x) * nc + c
-    some = lax.dynamic_slice(proj, (0, index * tall), (ny * lines, tall))
-    gram = lax.dot_general(some, proj, (((0,), (0,)), ((), ())), precision=HIGHEST)
+    chips = ny * nx
+    copies = jnp.broadcast_to(own, (chips, share, width))
+    proj = lax.all_to_all(copies, ("y", "x"), 0, 0, tiled=True)
+    tall = width // (chips * nc)
+    chip = y * nx + x
+    flat = proj.reshape(chips * share, width)
+    some = lax.dynamic_slice(flat, (0, chip * tall * nc), (chips * share, tall * nc))
+    gram = lax.dot_general(some, flat, (((0,), (0,)), ((), ())), precision=HIGHEST)
+    keep = lax.dynamic_slice(gram, (c * tall, 0), (tall, width))
+    give = lax.dynamic_slice(gram, ((1 - c) * tall, 0), (tall, width))
+    gram = keep + shift(give, "core", 1)
     copies = jnp.broadcast_to(gram, (nz, tall, width))
     gram = lax.all_to_all(copies, "z", 0, 0, tiled=True).sum(axis=0)
-    copies = jnp.broadcast_to(gram, (ny * nx, tall, width))
+    copies = jnp.broadcast_to(gram, (chips, tall, width))
     gram = lax.all_to_all(copies, ("y", "x"), 0, 0, tiled=True)
     other = shift(gram, "core", 1)
-    even = jnp.where(c == 0, gram, other)
-    odd = jnp.where(c == 0, other, gram)
-    gram = jnp.stack([even, odd], axis=1).reshape(width, width)
-    row = x * nc + c
-    root, right = polar(row.reshape(1), gram, here, width // nrow)
-    root = lax.dynamic_slice(root, (0, (y * nz + z) * (width // ncol)), (width // nrow, width // ncol))
-    return (root, right)
+    here = lax.dynamic_slice(proj, (y * nx, 0, 0), (nx, share, width))
+    there = shift(here, "core", 1)
+    where = jnp.stack([x * nc + c, c, y * nz + z]).astype(jnp.int32)
+    return polar(where, gram, other, here, there, (width // nrow, width // ncol))
 
 
 def solution(mesh):

time: 155 us -> 142 us (0.916)
  blocking collectives: 54.1 us -> 39.2 us
  waiting for transfers between devices: 14.4 us -> 27.4 us
  Pallas kernels: 29.1 us -> 23.5 us
  starting transfers between devices: 46.7 us -> 41.5 us
  other arithmetic: 2.93 us -> 0.24 us
  local copies, waits for them, and re-layouts: 6.62 us -> 8.65 us
    all_to_all x1 -> x0, blocking collectives: 10.4 us -> none  [local(): mine = lax.all_to_all(copies, ('y', 'x'), 0, 0, tiled=True)]
    ppermute x20 -> x21, starting transfers between devices: 46.7 us -> 38 us  [shift(): lax.ppermute(value, axis, [(i, (i + by) % size) for i in range(size)])]
    all_to_all x0 -> x1, waiting for transfers between devices: none -> 7.49 us  [local(): proj = lax.all_to_all(copies, ('y', 'x'), 0, 0, tiled=True)]
    ppermute x20 -> x21, waiting for transfers between devices: 14.4 us -> 19.9 us  [shift(): lax.ppermute(value, axis, [(i, (i + by) % size) for i in range(size)])]
    all_to_all x0 -> x1, starting transfers between devices: none -> 3.53 us  [local(): proj = lax.all_to_all(copies, ('y', 'x'), 0, 0, tiled=True)]
    all_to_all x1, blocking collectives: 15.2 us -> 12.5 us  [local(): tiles = lax.all_to_all(total, ('y', 'x'), 0, 0, tiled=True)]
    pallas_call x1, Pallas kernels: 3.03 us -> 0.96 us  [local(): pl.pallas_call(functools.partial(last_kernel, offsets, nz, share), out_sh...]
    all_to_all x1, blocking collectives: 16.1 us -> 14.1 us  [local(): gram = lax.all_to_all(copies, 'z', 0, 0, tiled=True).sum(axis=0)]
  transfers between devices with their start and end apart: 20 -> 22, of which waited for: 11 -> 12; matrix products, arithmetic and copies ran while one was open for 2% -> 2% of each run, Pallas kernels for 5% -> 3%
where the time goes in v2:
time: 142 us
  starting transfers between devices  41.5 us (29%)
  blocking collectives  39.2 us (28%)
  waiting for transfers between devices  27.4 us (19%)
  Pallas kernels  23.5 us (17%)
  local copies, waits for them, and re-layouts  8.65 us (6%)
    ppermute x21, starting transfers between devices, shift(): lax.ppermute(value, axis, [(i, (i + by) % size) for i in range(size)])  38 us
    ppermute x21, waiting for transfers between devices, shift(): lax.ppermute(value, axis, [(i, (i + by) % size) for i in range(size)])  19.9 us
    pallas_call x1, Pallas kernels, polar(): pl.pallas_call(polar_kernel, out_shape=(f32(short, height), f32(lines, wi...  17.6 us
    all_to_all x1, blocking collectives, local(): gram = lax.all_to_all(copies, 'z', 0, 0, tiled=True).sum(axis=0)  14.1 us
    all_to_all x1, blocking collectives, local(): gram = lax.all_to_all(copies, ('y', 'x'), 0, 0, tiled=True)  12.5 us
    all_to_all x1, blocking collectives, local(): tiles = lax.all_to_all(total, ('y', 'x'), 0, 0, tiled=True)  12.5 us
    all_to_all x1, waiting for transfers between devices, local(): proj = lax.all_to_all(copies, ('y', 'x'), 0, 0, tiled=True)  7.49 us
    all_to_all x1, starting transfers between devices, local(): proj = lax.all_to_all(copies, ('y', 'x'), 0, 0, tiled=True)  3.53 us
  transfers between devices with their start and end apart: 22, of which 12 were waited for; matrix products, arithmetic and copies ran while one was open for 2% of the time, Pallas kernels for 3%

profile of v2, /device:TPU:1, one launch (start us, length us, event | category | flops | bytes accessed | tf_op | source)
XLA Modules:
  0.0 141.7 jit_solution(7018125632576626515)
XLA Ops:
  0.6 0.0 copy-start
  0.6 1.9 %fusion.3 = (f32[128,512]{1,0:T(8,128)}, f32[128,512]{1,0:T(8,128)S(1)}) fusion(f32[256,512]{1,0:T(8,128)} %own.1), kind=kLoop, calls=%fused_computation.13 | loop fusion | bytes 1048576 | tf_op jit(solution)/shard_map/slice | solution.py:169
  2.6 6.4 %collective-permute-start.2 = (f32[128,512]{1,0:T(8,128)S(1)}, f32[128,512]{1,0:T(8,128)S(1)}, u32[]{:S(2)}, u32[]{:S(2)}) collective-permute-start(f32[128,512]{1,0:T(8,128)S(1)} %get-tuple-element.25), channel_id=1, source_target_pairs={{0,7},{1,0},{2,1},{3,2},{4,3},{5,4},{6,5},{7,6},{8,15},{9,8},{10,9... | collective-permute-start | bytes 786440 | tf_op jit(solution)/shard_map/ppermute | solution.py:17
  9.0 0.0 collective-permute-start
  9.0 0.0 collective-permute-start.4
  9.0 2.7 %collective-permute-start.7 = (f32[128,512]{1,0:T(8,128)}, f32[128,512]{1,0:T(8,128)}, u32[]{:S(2)}, u32[]{:S(2)}) collective-permute-start(f32[128,512]{1,0:T(8,128)} %get-tuple-element.24), channel_id=1, source_target_pairs={{0,7},{1,0},{2,1},{3,2},{4,3},{5,4},{6,5},{7,6},{8,15},{9,8},{10,9... | collective-permute-start | bytes 786440 | tf_op jit(solution)/shard_map/ppermute | solution.py:17
  11.7 2.3 %collective-permute-done.2.rest_0_ = f32[128,512]{1,0:T(8,128)S(1)} collective-permute-done((f32[128,512]{1,0:T(8,128)S(1)}, f32[128,512]{1,0:T(8,128)S(1)}, u32[]{:S(2)}, u32[]{:S(2)}) %collective-permute-start.2) | collective-permute-done | bytes 262176 | tf_op jit(solution)/shard_map/ppermute | solution.py:17
  14.0 3.2 %collective-permute-done.rest_2_ = f32[128,512]{1,0:T(8,128)} collective-permute-done((f32[128,512]{1,0:T(8,128)S(1)}, f32[128,512]{1,0:T(8,128)}, u32[]{:S(2)}, u32[]{:S(2)}) %collective-permute-start) | collective-permute-done | bytes 262176 | tf_op jit(solution)/shard_map/ppermute | solution.py:17
  17.2 0.0 collective-permute-start.1
  17.2 0.8 constant_dynamic-slice_fusion.4
  18.0 2.7 %collective-permute-start.3 = (f32[64,2048]{1,0:T(8,128)}, f32[64,2048]{1,0:T(8,128)S(1)}, u32[]{:S(2)}, u32[]{:S(2)}) collective-permute-start(f32[64,2048]{1,0:T(8,128)} %constant_dynamic-slice_fusion.4), channel_id=1, source_target_pairs={{0,24},{8,0},{16,8},{24,16},{1,25},{9,1},{17,9},{25,17},{2,26},{10... | collective-permute-start | bytes 1572872 | tf_op jit(solution)/shard_map/ppermute | solution.py:17
  20.8 2.0 %collective-permute-done.4.rest_3_ = f32[128,512]{1,0:T(8,128)} collective-permute-done((f32[128,512]{1,0:T(8,128)}, f32[128,512]{1,0:T(8,128)}, u32[]{:S(2)}, u32[]{:S(2)}) %collective-permute-start.4) | collective-permute-done | bytes 262176 | tf_op jit(solution)/shard_map/ppermute | solution.py:17
  22.8 0.0 collective-permute-start.10
  22.8 0.8 constant_dynamic-slice_fusion.3
  23.6 2.9 %collective-permute-start.5 = (f32[64,2048]{1,0:T(8,128)}, f32[64,2048]{1,0:T(8,128)}, u32[]{:S(2)}, u32[]{:S(2)}) collective-permute-start(f32[64,2048]{1,0:T(8,128)} %constant_dynamic-slice_fusion.3), channel_id=1, source_target_pairs={{0,16},{8,24},{16,0},{24,8},{1,17},{9,25},{17,1},{25,9},{2,18},{10... | collective-permute-start | bytes 1572872 | tf_op jit(solution)/shard_map/ppermute | solution.py:17
  26.6 0.0 collective-permute-done.7.rest_1_
  26.6 2.7 %collective-permute-start.8 = (f32[128,512]{1,0:T(8,128)S(1)}, f32[128,512]{1,0:T(8,128)S(1)}, u32[]{:S(2)}, u32[]{:S(2)}) collective-permute-start(f32[128,512]{1,0:T(8,128)S(1)} %collective-permute-done.2.rest_0_), channel_id=1, source_target_pairs={{0,7},{1,0},{2,1},{3,2},{4,3},{5,4},{6,5},{7,6},{8,15},{9,8},{10,9... | collective-permute-start | bytes 786440 | tf_op jit(solution)/shard_map/ppermute | solution.py:17
  29.2 0.0 collective-permute-done.1.rest_6_
  29.2 0.1 collective-permute-start.9
  29.3 0.8 constant_dynamic-slice_fusion.2
  30.2 3.9 %collective-permute-done.10.rest_7_ = f32[128,512]{1,0:T(8,128)S(1)} collective-permute-done((f32[128,512]{1,0:T(8,128)}, f32[128,512]{1,0:T(8,128)S(1)}, u32[]{:S(2)}, u32[]{:S(2)}) %collective-permute-start.10) | collective-permute-done | bytes 262176 | tf_op jit(solution)/shard_map/ppermute | solution.py:17
  34.0 1.2 collective-permute-start.6
  35.2 0.0 collective-permute-done.8.rest_4_
  35.2 0.1 collective-permute-start.13
  35.3 0.6 copy-done.4
  35.9 0.9 collective-permute-done.9.rest_5_
  36.8 3.4 %collective-permute-start.12 = (f32[128,512]{1,0:T(8,128)}, f32[128,512]{1,0:T(8,128)}, u32[]{:S(2)}, u32[]{:S(2)}) collective-permute-start(f32[128,512]{1,0:T(8,128)} %collective-permute-done.9.rest_5_), channel_id=1, source_target_pairs={{0,7},{1,0},{2,1},{3,2},{4,3},{5,4},{6,5},{7,6},{8,15},{9,8},{10,9... | collective-permute-start | bytes 786440 | tf_op jit(solution)/shard_map/ppermute | solution.py:17
  40.2 0.1 pad_add_fusion.1.at
  40.3 0.0 collective-permute-done.3.q1
  40.3 0.0 collective-permute-start.11
  40.4 0.0 collective-permute-done.5.q2
  40.4 1.4 %collective-permute-start.14 = (f32[128,512]{1,0:T(8,128)}, f32[128,512]{1,0:T(8,128)S(1)}, u32[]{:S(2)}, u32[]{:S(2)}) collective-permute-start(f32[128,512]{1,0:T(8,128)} %copy-done.2), channel_id=1, source_target_pairs={{0,1},{1,2},{2,3},{3,4},{4,5},{5,6},{6,7},{7,0},{8,9},{9,10},{10,1... | collective-permute-start | bytes 786440 | tf_op jit(solution)/shard_map/ppermute | solution.py:17
  41.8 0.5 collective-permute-done.13.rest_2_
  42.4 0.0 collective-permute-start.15
  42.4 1.5 %collective-permute-done.12.rest_1_ = f32[128,512]{1,0:T(8,128)} collective-permute-done((f32[128,512]{1,0:T(8,128)}, f32[128,512]{1,0:T(8,128)}, u32[]{:S(2)}, u32[]{:S(2)}) %collective-permute-start.12) | collective-permute-done | bytes 262176 | tf_op jit(solution)/shard_map/ppermute | solution.py:17
  43.9 3.4 %collective-permute-start.16 = (f32[128,512]{1,0:T(8,128)}, f32[128,512]{1,0:T(8,128)S(1)}, u32[]{:S(2)}, u32[]{:S(2)}) collective-permute-start(f32[128,512]{1,0:T(8,128)} %collective-permute-done.12.rest_1_), channel_id=1, source_target_pairs={{0,7},{1,0},{2,1},{3,2},{4,3},{5,4},{6,5},{7,6},{8,15},{9,8},{10,9... | collective-permute-start | bytes 786440 | tf_op jit(solution)/shard_map/ppermute | solution.py:17
  47.3 2.2 %collective-permute-done.6.q3 = f32[64,2048]{1,0:T(8,128)} collective-permute-done((f32[64,2048]{1,0:T(8,128)}, f32[64,2048]{1,0:T(8,128)}, u32[]{:S(2)}, u32[]{:S(2)}) %collective-permute-start.6) | collective-permute-done | bytes 524320 | tf_op jit(solution)/shard_map/ppermute | solution.py:17
  49.6 0.9 copy-done.3
  50.5 0.9 copy-done.5
  51.5 3.3 %first_chunks.1 = (f32[256,512]{1,0:T(8,128)S(1)}, bf16[256,2048]{1,0:T(8,128)(2,1)S(1)}, bf16[256,2048]{1,0:T(8,128)(2,1)S(1)}) custom-call(s32[3]{0:T(128)S(1)} %pad_add_fusion.1.at, f32[64,2048]{1,0:T(8,128)S(1)} %constant_dynamic-slice_fusion.5.q0, f32[64,2048]{1,0:T(8,128)S(1)} %collective-permute-done.3.q1, f32[64,2048]{1,0:T(8,128)} %collective-permute-done.5.q2, ...), custom_call_target="tpu_custom_call" | custom-call | flops 1006632960 | bytes 8388608 | tf_op jit(solution)/shard_map/first_chunks/pallas_call | solution.py:197
  54.8 0.0 collective-permute-done.11.rest_0_
  54.8 0.0 collective-permute-done.14.rest_3_
  54.8 1.6 %middle_chunks.1.before = f32[256,512]{1,0:T(8,128)S(1)} custom-call(s32[3]{0:T(128)S(1)} %pad_add_fusion.1.at, bf16[256,2048]{1,0:T(8,128)(2,1)S(1)} %get-tuple-element.17.high, bf16[256,2048]{1,0:T(8,128)(2,1)S(1)} %get-tuple-element.18.low, f32[256,512]{1,0:T(8,128)S(1)} %get-tuple-element.19.before, f32[128,512]{1,0:T(8,128)S(1)} %collective-permute-done.11.rest_0_, ...), custom_call_target="tpu_custom_call" | custom-call | flops 402653184 | bytes 4194304 | tf_op jit(solution)/shard_map/middle_chunks/pallas_call | solution.py:207
  56.5 0.0 collective-permute-done.16.rest_1_
  56.5 1.0 last_chunk.1
  57.5 5.5 %collective-permute-start.17 = (f32[128,512]{1,0:T(8,128)S(1)}, f32[128,512]{1,0:T(8,128)S(1)}, u32[]{:S(2)}, u32[]{:S(2)}) collective-permute-start(f32[128,512]{1,0:T(8,128)S(1)} %get-tuple-element.21), channel_id=1, source_target_pairs={{0,32},{32,0},{1,33},{33,1},{2,34},{34,2},{3,35},{35,3},{4,36},{36... | collective-permute-start | bytes 786440 | tf_op jit(solution)/shard_map/ppermute | solution.py:17
  63.0 1.2 collective-permute-done.17
  64.2 12.5 %all_to_all.20 = f32[16,8,512]{2,1,0:T(8,128)S(1)} all-to-all(f32[16,8,512]{2,1,0:T(8,128)S(1)} %add_bitcast_fusion), channel_id=1, replica_groups=mesh['x'=4,'core'=2,'y'=4,'z'=8] {'y','x'}, dimensions={0} | all-to-all | bytes 524288 | tf_op jit(solution)/shard_map/all_to_all | solution.py:229
  76.8 0.7 broadcast_in_dim.9
  77.5 3.5 %all-to-all-start.1 = ((f32[16,8,512]{2,1,0:T(8,128)}), f32[16,8,512]{2,1,0:T(8,128)S(1)}, u32[]{:S(2)}, u32[]{:S(2)}) async-start(f32[16,8,512]{2,1,0:T(8,128)} %broadcast_in_dim.9), calls=%async_computation.1 | async-start | bytes 524288 | tf_op jit(solution)/shard_map/all_to_all | solution.py:233
  81.1 7.5 %all-to-all-done.1 = f32[16,8,512]{2,1,0:T(8,128)S(1)} async-done(((f32[16,8,512]{2,1,0:T(8,128)}), f32[16,8,512]{2,1,0:T(8,128)S(1)}, u32[]{:S(2)}, u32[]{:S(2)}) %all-to-all-start.1) | async-done | bytes 262176 | tf_op jit(solution)/shard_map/all_to_all | solution.py:233
  88.6 0.3 fusion
  88.9 2.7 %collective-permute-start.18 = (f32[16,512]{1,0:T(8,128)S(1)}, f32[16,512]{1,0:T(8,128)S(1)}, u32[]{:S(2)}, u32[]{:S(2)}) collective-permute-start(f32[16,512]{1,0:T(8,128)S(1)} %constant_dynamic-slice_fusion.1), channel_id=1, source_target_pairs={{0,32},{32,0},{1,33},{33,1},{2,34},{34,2},{3,35},{35,3},{4,36},{36... | collective-permute-start | bytes 98312 | tf_op jit(solution)/shard_map/ppermute | solution.py:17
  91.7 0.9 collective-permute-done.18
  92.6 14.1 %all_to_all.21 = f32[8,16,512]{2,1,0:T(8,128)S(1)} all-to-all(f32[8,16,512]{2,1,0:T(8,128)S(1)} %broadcast_in_dim.10), channel_id=1, replica_groups=mesh['x'=4,'core'=2,'y'=4,'z'=8] {'z'}, dimensions={0} | all-to-all | bytes 524288 | tf_op jit(solution)/shard_map/all_to_all | solution.py:243
  106.7 0.1 broadcast_in_dim.11
  106.8 12.5 %all_to_all.22.mine_ref = f32[16,16,512]{2,1,0:T(8,128)S(1)} all-to-all(f32[16,16,512]{2,1,0:T(8,128)S(1)} %broadcast_in_dim.11), channel_id=1, replica_groups=mesh['x'=4,'core'=2,'y'=4,'z'=8] {'y','x'}, dimensions={0} | all-to-all | bytes 1048576 | tf_op jit(solution)/shard_map/all_to_all | solution.py:245
  119.3 2.6 %collective-permute-start.19 = (f32[16,16,512]{2,1,0:T(8,128)S(1)}, f32[16,16,512]{2,1,0:T(8,128)S(1)}, u32[]{:S(2)}, u32[]{:S(2)}) collective-permute-start(f32[16,16,512]{2,1,0:T(8,128)S(1)} %all_to_all.22.mine_ref), channel_id=1, source_target_pairs={{0,32},{32,0},{1,33},{33,1},{2,34},{34,2},{3,35},{35,3},{4,36},{36... | collective-permute-start | bytes 1572872 | tf_op jit(solution)/shard_map/ppermute | solution.py:17
  122.0 0.8 constant_dynamic-slice_fusion.here_ref
  122.8 0.0 collective-permute-start.20
  122.8 0.1 pad_add_fusion.at
  122.9 1.2 collective-permute-done.20.there_ref
  124.1 0.0 collective-permute-done.19.other_ref
  124.1 17.6 %polar.1 = (f32[16,64]{1,0:T(8,128)}, f32[64,512]{1,0:T(8,128)}) custom-call(s32[3]{0:T(128)S(1)} %pad_add_fusion.at, f32[16,16,512]{2,1,0:T(8,128)S(1)} %all_to_all.22.mine_ref, f32[16,16,512]{2,1,0:T(8,128)S(1)} %collective-permute-done.19.other_ref, f32[4,8,512]{2,1,0:T(8,128)S(1)} %constant_dynamic-slice_fusion.here_ref, ...), custom_call_target="tpu_custom_call" | custom-call | tf_op jit(solution)/shard_map/polar/pallas_call | solution.py:136
  (18 shorter events, 0.2 us)
Async XLA Ops:
  0.6 16.6 %copy-start = (f32[64,8192]{1,0:T(8,128)S(1)}, f32[64,8192]{1,0:T(8,128)}, u32[]{:S(2)}) copy-start(f32[64,8192]{1,0:T(8,128)} %param.2) | copy-start | bytes 6291460
  2.6 11.4 %collective-permute-start.2 = (f32[128,512]{1,0:T(8,128)S(1)}, f32[128,512]{1,0:T(8,128)S(1)}, u32[]{:S(2)}, u32[]{:S(2)}) collective-permute-start(f32[128,512]{1,0:T(8,128)S(1)} %get-tuple-element.25), channel_id=1, source_target_pairs={{0,7},{1,0},{2,1},{3,2},{4,3},{5,4},{6,5},{7,6},{8,15},{9,8},{10,9... | collective-permute-start | bytes 786440 | tf_op jit(solution)/shard_map/ppermute | solution.py:17
  9.0 8.2 %collective-permute-start = (f32[128,512]{1,0:T(8,128)S(1)}, f32[128,512]{1,0:T(8,128)}, u32[]{:S(2)}, u32[]{:S(2)}) collective-permute-start(f32[128,512]{1,0:T(8,128)S(1)} %get-tuple-element.25), channel_id=1, source_target_pairs={{0,1},{1,2},{2,3},{3,4},{4,5},{5,6},{6,7},{7,0},{8,9},{9,10},{10,1... | collective-permute-start | bytes 786440 | tf_op jit(solution)/shard_map/ppermute | solution.py:17
  9.0 13.8 %collective-permute-start.4 = (f32[128,512]{1,0:T(8,128)}, f32[128,512]{1,0:T(8,128)}, u32[]{:S(2)}, u32[]{:S(2)}) collective-permute-start(f32[128,512]{1,0:T(8,128)} %get-tuple-element.24), channel_id=1, source_target_pairs={{0,1},{1,2},{2,3},{3,4},{4,5},{5,6},{6,7},{7,0},{8,9},{9,10},{10,1... | collective-permute-start | bytes 786440 | tf_op jit(solution)/shard_map/ppermute | solution.py:17
  9.0 17.6 %collective-permute-start.7 = (f32[128,512]{1,0:T(8,128)}, f32[128,512]{1,0:T(8,128)}, u32[]{:S(2)}, u32[]{:S(2)}) collective-permute-start(f32[128,512]{1,0:T(8,128)} %get-tuple-element.24), channel_id=1, source_target_pairs={{0,7},{1,0},{2,1},{3,2},{4,3},{5,4},{6,5},{7,6},{8,15},{9,8},{10,9... | collective-permute-start | bytes 786440 | tf_op jit(solution)/shard_map/ppermute | solution.py:17
  11.7 37.9 %copy-start.1 = (f32[256,512]{1,0:T(8,128)S(1)}, f32[256,512]{1,0:T(8,128)}, u32[]{:S(2)}) copy-start(f32[256,512]{1,0:T(8,128)} %own.1) | copy-start | bytes 1572868
  17.2 12.0 %collective-permute-start.1 = (f32[128,512]{1,0:T(8,128)}, f32[128,512]{1,0:T(8,128)}, u32[]{:S(2)}, u32[]{:S(2)}) collective-permute-start(f32[128,512]{1,0:T(8,128)} %collective-permute-done.rest_2_), channel_id=1, source_target_pairs={{0,1},{1,2},{2,3},{3,4},{4,5},{5,6},{6,7},{7,0},{8,9},{9,10},{10,1... | collective-permute-start | bytes 786440 | tf_op jit(solution)/shard_map/ppermute | solution.py:17
  18.0 22.3 %collective-permute-start.3 = (f32[64,2048]{1,0:T(8,128)}, f32[64,2048]{1,0:T(8,128)S(1)}, u32[]{:S(2)}, u32[]{:S(2)}) collective-permute-start(f32[64,2048]{1,0:T(8,128)} %constant_dynamic-slice_fusion.4), channel_id=1, source_target_pairs={{0,24},{8,0},{16,8},{24,16},{1,25},{9,1},{17,9},{25,17},{2,26},{10... | collective-permute-start | bytes 1572872 | tf_op jit(solution)/shard_map/ppermute | solution.py:17
  22.8 11.2 %collective-permute-start.10 = (f32[128,512]{1,0:T(8,128)}, f32[128,512]{1,0:T(8,128)S(1)}, u32[]{:S(2)}, u32[]{:S(2)}) collective-permute-start(f32[128,512]{1,0:T(8,128)} %collective-permute-done.4.rest_3_), channel_id=1, source_target_pairs={{0,1},{1,2},{2,3},{3,4},{4,5},{5,6},{6,7},{7,0},{8,9},{9,10},{10,1... | collective-permute-start | bytes 786440 | tf_op jit(solution)/shard_map/ppermute | solution.py:17
  23.6 16.7 %collective-permute-start.5 = (f32[64,2048]{1,0:T(8,128)}, f32[64,2048]{1,0:T(8,128)}, u32[]{:S(2)}, u32[]{:S(2)}) collective-permute-start(f32[64,2048]{1,0:T(8,128)} %constant_dynamic-slice_fusion.3), channel_id=1, source_target_pairs={{0,16},{8,24},{16,0},{24,8},{1,17},{9,25},{17,1},{25,9},{2,18},{10... | collective-permute-start | bytes 1572872 | tf_op jit(solution)/shard_map/ppermute | solution.py:17
  26.6 8.7 %collective-permute-start.8 = (f32[128,512]{1,0:T(8,128)S(1)}, f32[128,512]{1,0:T(8,128)S(1)}, u32[]{:S(2)}, u32[]{:S(2)}) collective-permute-start(f32[128,512]{1,0:T(8,128)S(1)} %collective-permute-done.2.rest_0_), channel_id=1, source_target_pairs={{0,7},{1,0},{2,1},{3,2},{4,3},{5,4},{6,5},{7,6},{8,15},{9,8},{10,9... | collective-permute-start | bytes 786440 | tf_op jit(solution)/shard_map/ppermute | solution.py:17
  29.2 7.6 %collective-permute-start.9 = (f32[128,512]{1,0:T(8,128)}, f32[128,512]{1,0:T(8,128)}, u32[]{:S(2)}, u32[]{:S(2)}) collective-permute-start(f32[128,512]{1,0:T(8,128)} %collective-permute-done.7.rest_1_), channel_id=1, source_target_pairs={{0,7},{1,0},{2,1},{3,2},{4,3},{5,4},{6,5},{7,6},{8,15},{9,8},{10,9... | collective-permute-start | bytes 786440 | tf_op jit(solution)/shard_map/ppermute | solution.py:17
  34.0 1.2 copy-start.2
  34.0 15.5 %collective-permute-start.6 = (f32[64,2048]{1,0:T(8,128)}, f32[64,2048]{1,0:T(8,128)}, u32[]{:S(2)}, u32[]{:S(2)}) collective-permute-start(f32[64,2048]{1,0:T(8,128)} %constant_dynamic-slice_fusion.2), channel_id=1, source_target_pairs={{0,8},{8,16},{16,24},{24,0},{1,9},{9,17},{17,25},{25,1},{2,10},{10... | collective-permute-start | bytes 1572872 | tf_op jit(solution)/shard_map/ppermute | solution.py:17
  35.2 0.7 copy-start.4
  35.2 7.1 %collective-permute-start.13 = (f32[128,512]{1,0:T(8,128)}, f32[128,512]{1,0:T(8,128)}, u32[]{:S(2)}, u32[]{:S(2)}) collective-permute-start(f32[128,512]{1,0:T(8,128)} %collective-permute-done.1.rest_6_), channel_id=1, source_target_pairs={{0,1},{1,2},{2,3},{3,4},{4,5},{5,6},{6,7},{7,0},{8,9},{9,10},{10,1... | collective-permute-start | bytes 786440 | tf_op jit(solution)/shard_map/ppermute | solution.py:17
  36.8 7.0 %collective-permute-start.12 = (f32[128,512]{1,0:T(8,128)}, f32[128,512]{1,0:T(8,128)}, u32[]{:S(2)}, u32[]{:S(2)}) collective-permute-start(f32[128,512]{1,0:T(8,128)} %collective-permute-done.9.rest_5_), channel_id=1, source_target_pairs={{0,7},{1,0},{2,1},{3,2},{4,3},{5,4},{6,5},{7,6},{8,15},{9,8},{10,9... | collective-permute-start | bytes 786440 | tf_op jit(solution)/shard_map/ppermute | solution.py:17
  40.3 14.5 %collective-permute-start.11 = (f32[128,512]{1,0:T(8,128)}, f32[128,512]{1,0:T(8,128)S(1)}, u32[]{:S(2)}, u32[]{:S(2)}) collective-permute-start(f32[128,512]{1,0:T(8,128)} %copy-done.4), channel_id=1, source_target_pairs={{0,7},{1,0},{2,1},{3,2},{4,3},{5,4},{6,5},{7,6},{8,15},{9,8},{10,9... | collective-permute-start | bytes 786440 | tf_op jit(solution)/shard_map/ppermute | solution.py:17
  40.4 14.5 %collective-permute-start.14 = (f32[128,512]{1,0:T(8,128)}, f32[128,512]{1,0:T(8,128)S(1)}, u32[]{:S(2)}, u32[]{:S(2)}) collective-permute-start(f32[128,512]{1,0:T(8,128)} %copy-done.2), channel_id=1, source_target_pairs={{0,1},{1,2},{2,3},{3,4},{4,5},{5,6},{6,7},{7,0},{8,9},{9,10},{10,1... | collective-permute-start | bytes 786440 | tf_op jit(solution)/shard_map/ppermute | solution.py:17
  42.4 14.1 %collective-permute-start.15 = (f32[128,512]{1,0:T(8,128)}, f32[128,512]{1,0:T(8,128)S(1)}, u32[]{:S(2)}, u32[]{:S(2)}) collective-permute-start(f32[128,512]{1,0:T(8,128)} %collective-permute-done.13.rest_2_), channel_id=1, source_target_pairs={{0,1},{1,2},{2,3},{3,4},{4,5},{5,6},{6,7},{7,0},{8,9},{9,10},{10,1... | collective-permute-start | bytes 786440 | tf_op jit(solution)/shard_map/ppermute | solution.py:17
  43.9 12.6 %collective-permute-start.16 = (f32[128,512]{1,0:T(8,128)}, f32[128,512]{1,0:T(8,128)S(1)}, u32[]{:S(2)}, u32[]{:S(2)}) collective-permute-start(f32[128,512]{1,0:T(8,128)} %collective-permute-done.12.rest_1_), channel_id=1, source_target_pairs={{0,7},{1,0},{2,1},{3,2},{4,3},{5,4},{6,5},{7,6},{8,15},{9,8},{10,9... | collective-permute-start | bytes 786440 | tf_op jit(solution)/shard_map/ppermute | solution.py:17
  49.6 1.0 copy-start.3
  50.5 0.9 copy-start.5
  57.5 6.7 %collective-permute-start.17 = (f32[128,512]{1,0:T(8,128)S(1)}, f32[128,512]{1,0:T(8,128)S(1)}, u32[]{:S(2)}, u32[]{:S(2)}) collective-permute-start(f32[128,512]{1,0:T(8,128)S(1)} %get-tuple-element.21), channel_id=1, source_target_pairs={{0,32},{32,0},{1,33},{33,1},{2,34},{34,2},{3,35},{35,3},{4,36},{36... | collective-permute-start | bytes 786440 | tf_op jit(solution)/shard_map/ppermute | solution.py:17
  77.5 11.0 %all-to-all-start.1 = ((f32[16,8,512]{2,1,0:T(8,128)}), f32[16,8,512]{2,1,0:T(8,128)S(1)}, u32[]{:S(2)}, u32[]{:S(2)}) async-start(f32[16,8,512]{2,1,0:T(8,128)} %broadcast_in_dim.9), calls=%async_computation.1 | async-start | bytes 524288 | tf_op jit(solution)/shard_map/all_to_all | solution.py:233
  88.6 33.4 %copy-start.6 = (f32[16,8,512]{2,1,0:T(8,128)}, f32[16,8,512]{2,1,0:T(8,128)S(1)}, u32[]{:S(2)}) copy-start(f32[16,8,512]{2,1,0:T(8,128)S(1)} %all-to-all-done.1) | copy-start | bytes 786436
  88.9 3.6 %collective-permute-start.18 = (f32[16,512]{1,0:T(8,128)S(1)}, f32[16,512]{1,0:T(8,128)S(1)}, u32[]{:S(2)}, u32[]{:S(2)}) collective-permute-start(f32[16,512]{1,0:T(8,128)S(1)} %constant_dynamic-slice_fusion.1), channel_id=1, source_target_pairs={{0,32},{32,0},{1,33},{33,1},{2,34},{34,2},{3,35},{35,3},{4,36},{36... | collective-permute-start | bytes 98312 | tf_op jit(solution)/shard_map/ppermute | solution.py:17
  119.3 4.7 %collective-permute-start.19 = (f32[16,16,512]{2,1,0:T(8,128)S(1)}, f32[16,16,512]{2,1,0:T(8,128)S(1)}, u32[]{:S(2)}, u32[]{:S(2)}) collective-permute-start(f32[16,16,512]{2,1,0:T(8,128)S(1)} %all_to_all.22.mine_ref), channel_id=1, source_target_pairs={{0,32},{32,0},{1,33},{33,1},{2,34},{34,2},{3,35},{35,3},{4,36},{36... | collective-permute-start | bytes 1572872 | tf_op jit(solution)/shard_map/ppermute | solution.py:17
  122.8 1.3 collective-permute-start.20
